TPU v7x, 32 devices: a whole 2x2x4 slice. The times are simulated.
32 devices in a mesh: replica: 8 (over y, x, core), tensor: 4 (over z).
Axes of the slice: x: 2, y: 2, z: 4, core: 2. Of those that a mesh axis runs over, the one named last changes fastest.
Arguments:
- weights: bfloat16 [8, 7168, 2048], P('replica', 'tensor'), may hold values from -6 to 6
- hidden: bfloat16 [8, 2, 512, 7168], P('replica', None, None, 'tensor'), may hold values from -6 to 6
- targets: bfloat16 [8, 2, 512, 2048], P('replica'), may hold values from -6 to 6
- norm_gain: float32 [2048], replicated, may hold values from 0.5 to 2
- stragglers: int32 [2, 8], replicated, may hold values 0 or 1
Outputs:
- new_weights: bfloat16 [8, 7168, 2048], P('replica', 'tensor')
All inputs are finite; a program needn't handle non-finite values.
Results may differ from a plain program's by a relative error of at most 0.011.
Values may be sent and summed in bfloat16 or wider, within the bound.
A program may use at most 128 MiB of HBM per device.

v0:
```python
import functools

import jax
import jax.numpy as jnp
from jax import lax
from jax.experimental import pallas as pl
from jax.experimental.pallas import tpu as pltpu
from jax.sharding import PartitionSpec as P

FF = 7168
STEPS = 2


eps = 1e-05
learn_rate = 0.5

MESH = pl.DeviceIdType.MESH
TILE = 256
ROWS = 256
AHEAD = 2
BESIDE = 5


def contract_rows(left, right):
    return lax.dot_general(
        left, right, (((0,), (0,)), ((), ())), preferred_element_type=jnp.float32
    )


def norm_backward(outputs, target_rows, norm_gain):
    squares = jnp.mean(outputs * outputs, axis=-1, keepdims=True)
    inverse = lax.rsqrt(squares + eps)
    normed = outputs * inverse
    weighted = (normed * norm_gain - target_rows.astype(jnp.float32)) * norm_gain
    cross_mean = jnp.mean(weighted * normed, axis=-1, keepdims=True)
    return (inverse * (weighted - normed * cross_mean)).astype(jnp.bfloat16)


def step_kernel(apart, last, *refs):
    hidden_ref, weight_ref, target_ref, gain_ref, mix_ref, cargo_ref, new_ref = refs[:7]
    if last:
        landed_ref, rest = refs[7], refs[8:]
        cargo_from, paired_hidden_ref = weight_ref, cargo_ref
    else:
        landed_ref, rest = refs[7], refs[8:]
        cargo_from = cargo_ref
    grad_ref, terms, in_right, in_left, out_right, out_left = rest[:6]
    right_send, right_recv, left_send, left_recv, cargo_send, cargo_recv = rest[6:12]
    if last:
        far_grad, grad_send, grad_recv, share_send, share_recv = rest[12:]
    else:
        mine_ref, theirs_ref, near_send, near_recv = rest[12:]

    count = lax.axis_size("tensor")
    me = lax.axis_index("tensor")
    replica = lax.axis_index("replica")
    step = 1 << apart
    far = replica + step - 2 * step * ((replica // step) % 2)
    last_rank = count - 1
    factor = FF ** (-0.5)

    barrier = pltpu.get_barrier_semaphore()
    pl.semaphore_signal(barrier, inc=1, device_id=(far, me), device_id_type=MESH)
    for hop in range(1, count):
        peer = lax.rem(me + hop, count)
        pl.semaphore_signal(barrier, inc=1, device_id=(replica, peer), device_id_type=MESH)
    near = replica + 1 - 2 * (replica % 2)
    if not last:
        pl.semaphore_signal(barrier, inc=1, device_id=(near, me), device_id_type=MESH)
    pl.semaphore_wait(barrier, count if last else count + 1)

    pieces = cargo_send.shape[0]
    depth = cargo_from.shape[0] // pieces

    def cargo(index):
        span = pl.ds(index * depth, depth)
        return pltpu.make_async_remote_copy(
            src_ref=cargo_from.at[span], dst_ref=landed_ref.at[span],
            send_sem=cargo_send.at[index], recv_sem=cargo_recv.at[index],
            device_id=(far, me), device_id_type=MESH,
        )

    for index in range(AHEAD):
        cargo(index).start()

    @pl.when(me == 0)
    def _():
        in_right[...] = jnp.zeros_like(in_right)

    @pl.when(me == last_rank)
    def _():
        in_left[...] = jnp.zeros_like(in_left)

    tiles, tokens = terms.shape[0], terms.shape[1]
    halves = tokens // ROWS
    chunks = tiles * halves

    def place(chunk):
        return chunk // halves, pl.ds(pl.multiple_of((chunk % halves) * ROWS, ROWS), ROWS)

    def right_copy(chunk):
        tile, rows = place(chunk)
        return pltpu.make_async_remote_copy(
            src_ref=out_right.at[tile, rows], dst_ref=in_right.at[tile, rows],
            send_sem=right_send.at[chunk], recv_sem=right_recv.at[chunk],
            device_id=(replica, lax.rem(me + 1, count)), device_id_type=MESH,
        )

    def left_copy(chunk):
        tile, rows = place(chunk)
        return pltpu.make_async_remote_copy(
            src_ref=out_left.at[tile, rows], dst_ref=in_left.at[tile, rows],
            send_sem=left_send.at[chunk], recv_sem=left_recv.at[chunk],
            device_id=(replica, lax.rem(me + count - 1, count)), device_id_type=MESH,
        )

    def turn(now, _):
        @pl.when(now < chunks)
        def _():
            tile, rows = place(now)
            columns = pl.ds(pl.multiple_of(tile * TILE, TILE), TILE)
            terms[tile, rows, :] = factor * jnp.dot(
                hidden_ref[rows, :], weight_ref[:, columns], preferred_element_type=jnp.float32
            )

        rightward = now - me

        @pl.when((rightward >= 0) & (rightward < chunks))
        def _():
            @pl.when(me > 0)
            def _():
                right_copy(rightward).wait_recv()

            @pl.when(me < last_rank)
            def _():
                tile, rows = place(rightward)
                total = terms[tile, rows, :] + in_right[tile, rows, :].astype(jnp.float32)
                out_right[tile, rows, :] = total.astype(jnp.bfloat16)
                right_copy(rightward).start()

        leftward = now - (last_rank - me)

        @pl.when((leftward >= 0) & (leftward < chunks))
        def _():
            @pl.when(me < last_rank)
            def _():
                left_copy(leftward).wait_recv()

            @pl.when(me > 0)
            def _():
                tile, rows = place(leftward)
                total = terms[tile, rows, :] + in_left[tile, rows, :].astype(jnp.float32)
                out_left[tile, rows, :] = total.astype(jnp.bfloat16)
                left_copy(leftward).start()

        if last:
            pace = (chunks + last_rank) // (BESIDE - AHEAD)
            index = AHEAD + now // pace

            @pl.when((now % pace == pace - 1) & (index < BESIDE))
            def _():
                cargo(index).start()

        return 0

    if not last:
        for index in range(AHEAD, pieces):
            cargo(index).start()
    lax.fori_loop(0, chunks + last_rank, turn, 0)

    block = 32

    def normalise(index, _):
        rows = pl.ds(pl.multiple_of(index * block, block), block)
        outputs = jnp.concatenate(
            [
                terms[tile, rows, :]
                + in_right[tile, rows, :].astype(jnp.float32)
                + in_left[tile, rows, :].astype(jnp.float32)
                for tile in range(tiles)
            ],
            axis=1,
        )
        grad_ref[rows, :] = norm_backward(outputs, target_ref[rows, :], gain_ref[...])
        return 0

    lax.fori_loop(0, tokens // block, normalise, 0)

    if last:
        part = tokens // count
        mine = pl.ds(pl.multiple_of(me * part, part), part)
        across = pltpu.make_async_remote_copy(
            src_ref=grad_ref.at[mine], dst_ref=far_grad.at[mine],
            send_sem=grad_send, recv_sem=grad_recv,
            device_id=(far, me), device_id_type=MESH,
        )
        across.start()
        for index in range(BESIDE, pieces):
            cargo(index).start()
        across.wait_recv()

        def share(hop):
            return pltpu.make_async_remote_copy(
                src_ref=far_grad.at[mine], dst_ref=far_grad.at[mine],
                send_sem=share_send.at[hop - 1], recv_sem=share_recv.at[hop - 1],
                device_id=(replica, lax.rem(me + hop, count)), device_id_type=MESH,
            )

        for hop in range(1, count):
            share(hop).start()
        for hop in range(1, count):
            share(hop).wait_recv()
        for hop in range(1, count):
            share(hop).wait_send()
        across.wait_send()

    def drain(chunk, _):
        @pl.when(me < last_rank)
        def _():
            right_copy(chunk).wait_send()

        @pl.when(me > 0)
        def _():
            left_copy(chunk).wait_send()

        return 0

    lax.fori_loop(0, chunks, drain, 0)

    def descended(block_ref, rows_ref, gradient_ref, rows):
        grad_weight = (factor * contract_rows(rows_ref[:, rows], gradient_ref[...])).astype(
            jnp.bfloat16
        )
        return (
            block_ref[rows, :].astype(jnp.float32) - learn_rate * grad_weight.astype(jnp.float32)
        ).astype(jnp.bfloat16)

    def mix(own, other):
        return (
            own.astype(jnp.float32) * mix_ref[0] + other.astype(jnp.float32) * mix_ref[1]
        ).astype(jnp.bfloat16)

    if last:

        def finish(index, _):
            rows = pl.ds(pl.multiple_of(index * depth, depth), depth)
            own = descended(weight_ref, hidden_ref, grad_ref, rows)
            cargo(index).wait_recv()
            other = descended(landed_ref, paired_hidden_ref, far_grad, rows)
            new_ref[rows, :] = mix(own, other)
            return 0

        lax.fori_loop(0, pieces, finish, 0)
        for index in range(pieces):
            cargo(index).wait_send()
    else:
        slabs = near_send.shape[0]
        height = weight_ref.shape[0] // slabs

        def near_copy(slab):
            rows = pl.ds(pl.multiple_of(slab * height, height), height)
            return pltpu.make_async_remote_copy(
                src_ref=mine_ref.at[rows], dst_ref=theirs_ref.at[rows],
                send_sem=near_send.at[slab], recv_sem=near_recv.at[slab],
                device_id=(near, me), device_id_type=MESH,
            )

        def offer(slab, _):
            rows = pl.ds(pl.multiple_of(slab * height, height), height)
            mine_ref[rows, :] = descended(weight_ref, hidden_ref, grad_ref, rows)
            near_copy(slab).start()
            return 0

        def settle(slab, _):
            rows = pl.ds(pl.multiple_of(slab * height, height), height)
            near_copy(slab).wait_recv()
            new_ref[rows, :] = mix(mine_ref[rows, :], theirs_ref[rows, :])
            return 0

        def sent(slab, _):
            near_copy(slab).wait_send()
            return 0

        lax.fori_loop(0, slabs, offer, 0)
        lax.fori_loop(0, slabs, settle, 0)
        lax.fori_loop(0, slabs, sent, 0)
        for index in range(pieces):
            cargo(index).wait()


def run_step(hidden_rows, weight_block, target_rows, norm_gain, weighing, cargo, apart, last):
    tokens, features = target_rows.shape
    tiles = features // TILE
    chunks = tiles * (tokens // ROWS)
    count = lax.axis_size("tensor")
    vmem = pl.BlockSpec(memory_space=pltpu.VMEM)
    smem = pl.BlockSpec(memory_space=pltpu.SMEM)
    anywhere = pl.BlockSpec(memory_space=pl.ANY)
    pieces = weight_block.shape[0] // 128 if last else tokens // 32
    slabs = weight_block.shape[0] // 256
    gradient = pltpu.VMEM((tokens, features), jnp.bfloat16)
    stacked = jax.ShapeDtypeStruct(weight_block.shape, weight_block.dtype)
    whole = pltpu.VMEM(weight_block.shape, weight_block.dtype)
    travelling = pltpu.VMEM((tiles, tokens, TILE), jnp.bfloat16)
    scratch = [whole] if last else []
    scratch += [gradient, pltpu.VMEM((tiles, tokens, TILE), jnp.float32)] + [travelling] * 4
    scratch += [pltpu.SemaphoreType.DMA((chunks,))] * 4 + [pltpu.SemaphoreType.DMA((pieces,))] * 2
    if last:
        scratch += [gradient]
        scratch += [pltpu.SemaphoreType.DMA] * 2 + [pltpu.SemaphoreType.DMA((count - 1,))] * 2
        out_shape, out_specs = stacked, vmem
    else:
        scratch += [whole] * 2 + [pltpu.SemaphoreType.DMA((slabs,))] * 2
        out_shape = (stacked, jax.ShapeDtypeStruct(cargo.shape, cargo.dtype))
        out_specs = (vmem, anywhere)
    return pl.pallas_call(
        functools.partial(step_kernel, apart, last),
        out_shape=out_shape,
        in_specs=[vmem] * 4 + [smem] + [vmem if last else anywhere],
        out_specs=out_specs,
        scratch_shapes=scratch,
        compiler_params=pltpu.CompilerParams(
            collective_id=int(last), has_side_effects=True, vmem_limit_bytes=63 << 20
        ),
    )(hidden_rows, weight_block, target_rows, norm_gain[None], weighing, cargo)


def on_device(weights, hidden, targets, norm_gain, stragglers):
    replica_index = lax.axis_index("replica")
    weight_block = weights[0]

    def weighing(update_step):
        partner_index = jnp.bitwise_xor(replica_index, jnp.int32(1 << update_step))
        mask_row = stragglers[update_step]
        self_late = lax.dynamic_index_in_dim(mask_row, replica_index, keepdims=False)
        partner_late = lax.dynamic_index_in_dim(mask_row, partner_index, keepdims=False)
        keep_pair = (self_late == 0) & (partner_late == 0)
        return jnp.where(keep_pair, jnp.array([0.5, 0.5]), jnp.array([1.0, 0.0]))

    first, second = hidden[0, 0], hidden[0, 1]
    weight_block, paired_hidden = run_step(
        first, weight_block, targets[0, 0], norm_gain, weighing(0), second, 1, False
    )
    return run_step(
        second, weight_block, targets[0, 1], norm_gain, weighing(1), paired_hidden, 1, True
    )[None]


def solution(mesh):
    placed = (
        P("replica", "tensor", None),
        P("replica", None, None, "tensor"),
        P("replica", None, None, None),
        P(),
        P(),
    )
    return jax.shard_map(
        on_device,
        mesh=mesh,
        in_specs=placed,
        out_specs=P("replica", "tensor", None),
        check_vma=False,
    )
```

profile of v0, /device:TPU:0, one launch (start us, length us, event | category | flops | bytes accessed | tf_op | source)
XLA Modules:
  0.0 324.7 jit_solution(12400766380929260431)
XLA Ops:
  0.0 0.8 fusion
  0.8 0.7 constant_dynamic-slice_fusion
  4.0 1.2 broadcast_select_fusion
  5.3 0.0 copy-start
  5.3 4.2 %slice_bitcast_fusion.2 = (bf16[512,1792]{1,0:T(8,128)(2,1)}, bf16[512,1792]{1,0:T(8,128)(2,1)}) fusion(bf16[1,2,512,1792]{3,2,1,0:T(8,128)(2,1)} %param.10), kind=kLoop, calls=%fused_computation.2 | loop fusion | bytes 7340032 | tf_op jit(solution)/shard_map/squeeze | solution.py:340
  9.5 0.0 copy-done
  9.5 2.6 slice_bitcast_fusion
  12.1 106.1 %shard_map.91 = (bf16[1792,2048]{1,0:T(8,128)(2,1)}, bf16[512,1792]{1,0:T(8,128)(2,1)}) custom-call(bf16[512,1792]{1,0:T(8,128)(2,1)} %get-tuple-element.11.refs_0_, bf16[1792,2048]{1,0:T(8,128)(2,1)} %bitcast.14, bf16[512,2048]{1,0:T(8,128)(2,1)} %get-tuple-element.10.refs_2_, f32[1,2048]{1,0:T(1,128)} %bitcast.15, f32[2]{0:T(128)} %get-tuple-element.16.refs_4_, ...), custom_call_target="tpu_custom_call" | custom-call | tf_op jit(solution)/shard_map/pallas_call | solution.py:316
  118.2 199.0 %shard_map.92 = bf16[1792,2048]{1,0:T(8,128)(2,1)} custom-call(bf16[512,1792]{1,0:T(8,128)(2,1)} %get-tuple-element.12.refs_5_.refs_0_, bf16[1792,2048]{1,0:T(8,128)(2,1)} %get-tuple-element.7.refs_1_, bf16[512,2048]{1,0:T(8,128)(2,1)} %get-tuple-element.9.refs_2_, f32[1,2048]{1,0:T(1,128)} %bitcast.16, f32[2]{0:T(128)} %get-tuple-element.15.refs_4_, ...), custom_call_target="tpu_custom_call" | custom-call | tf_op jit(solution)/shard_map/pallas_call | solution.py:316
  317.2 7.5 %copy.11 = bf16[1,1792,2048]{2,1,0:T(8,128)(2,1)} copy(bf16[1,1792,2048]{2,1,0:T(8,128)(2,1)} %bitcast.13) | data formatting | bytes 14680064
Async XLA Ops:
  5.3 4.2 %copy-start = (bf16[1,2,512,2048]{3,2,1,0:T(8,128)(2,1)S(1)}, bf16[1,2,512,2048]{3,2,1,0:T(8,128)(2,1)}, u32[]{:S(2)}) copy-start(bf16[1,2,512,2048]{3,2,1,0:T(8,128)(2,1)} %param.11) | copy-start | bytes 12582916
where the time goes:
time: 325 us
  Pallas kernels  305 us (94%)
  local copies, waits for them, and re-layouts  15.8 us (5%)
    pallas_call x2, Pallas kernels, run_step(): pl.pallas_call(functools.partial(step_kernel, apart, last), out_shape=out...  305 us
    unnamed x3, local copies, waits for them, and re-layouts  7.53 us

commit v1 on v0

v1 whole, which is shorter than its diff:
```python
import functools

import jax
import jax.numpy as jnp
from jax import lax
from jax.experimental import pallas as pl
from jax.experimental.pallas import tpu as pltpu
from jax.sharding import PartitionSpec as P

eps = 1e-05
learn_rate = 0.5

MESH = pl.DeviceIdType.MESH
TILE = 512
ROWS = 128
SLAB = 128
MIDDLE = 4 / 14
EARLY = 3 / 14


def contract_rows(left, right):
    return lax.dot_general(
        left, right, (((0,), (0,)), ((), ())), preferred_element_type=jnp.float32
    )


def norm_backward(outputs, target_rows, norm_gain):
    squares = jnp.mean(outputs * outputs, axis=-1, keepdims=True)
    inverse = lax.rsqrt(squares + eps)
    normed = outputs * inverse
    weighted = (normed * norm_gain - target_rows.astype(jnp.float32)) * norm_gain
    cross_mean = jnp.mean(weighted * normed, axis=-1, keepdims=True)
    return (inverse * (weighted - normed * cross_mean)).astype(jnp.bfloat16)


def flip(index, bit):
    return index + bit - 2 * bit * ((index // bit) % 2)


def steps_kernel(middle, early, *refs):
    weights_ref, hidden_ref, targets_ref, gain_ref, late_ref, new_ref = refs[:6]
    own, theirs, far_own, crossed, rows_in, far_first, far_second = refs[6:13]
    goal, terms, arriving, out_right, out_left, grads, far_grads = refs[13:20]
    tile_load, load, right_send, right_recv, left_send, left_recv = refs[20:26]
    near_send, near_recv, cargo_send, cargo_recv, swap_send, swap_recv = refs[26:32]
    side_send, side_recv, across_send, across_recv = refs[32:36]
    share_right, share_left, share_recv, store_sem = refs[36:]

    count = lax.axis_size("tensor")
    me = lax.axis_index("tensor")
    replica = lax.axis_index("replica")
    last = count - 1
    near, far = flip(replica, 1), flip(replica, 2)
    cross = flip(near, 2)
    depth, features = own.shape
    tokens = grads.shape[1]
    tiles = terms.shape[0]
    blocks = tokens // ROWS
    chunks = tiles * blocks
    slabs = depth // SLAB
    ready = middle + early
    factor = (depth * count) ** (-0.5)

    def share_of(step, one, other):
        late = (late_ref[step, one] != 0) | (late_ref[step, other] != 0)
        return jnp.where(late, 1.0, 0.5), jnp.where(late, 0.0, 0.5)

    own_mix = share_of(0, replica, near)
    far_mix = share_of(0, far, cross)
    end_mix = share_of(1, replica, far)

    def mix(shares, one, other):
        return (
            one.astype(jnp.float32) * shares[0] + other.astype(jnp.float32) * shares[1]
        ).astype(jnp.bfloat16)

    def columns_of(tile):
        return pl.ds(pl.multiple_of(tile * TILE, TILE), TILE)

    def tile_copy(tile):
        span = columns_of(tile)
        return pltpu.make_async_copy(
            weights_ref.at[0, :, span], own.at[:, span], tile_load.at[tile]
        )

    def hidden_copy(step):
        return pltpu.make_async_copy(hidden_ref.at[0, step], rows_in.at[step], load.at[step, 0])

    def target_copy(step):
        return pltpu.make_async_copy(targets_ref.at[0, step], goal.at[step], load.at[step, 1])

    hidden_copy(0).start()
    for tile in range(tiles):
        tile_copy(tile).start()
    target_copy(0).start()
    hidden_copy(1).start()
    target_copy(1).start()

    barrier = pltpu.get_barrier_semaphore()
    pl.semaphore_signal(barrier, inc=1, device_id=(far, me), device_id_type=MESH)
    pl.semaphore_signal(barrier, inc=1, device_id=(near, me), device_id_type=MESH)
    for hop in range(1, count):
        peer = lax.rem(me + hop, count)
        pl.semaphore_signal(barrier, inc=1, device_id=(replica, peer), device_id_type=MESH)
    pl.semaphore_wait(barrier, count + 1)

    def slab_rows(slab):
        return pl.ds(pl.multiple_of(slab * SLAB, SLAB), SLAB)

    def remote(source, target, send, recv, device):
        return pltpu.make_async_remote_copy(
            src_ref=source, dst_ref=target, send_sem=send, recv_sem=recv,
            device_id=device, device_id_type=MESH,
        )

    def early_cargo(slab):
        span = slab_rows(slab)
        return remote(
            weights_ref.at[0, span], far_own.at[span],
            cargo_send.at[slab], cargo_recv.at[slab], (far, me),
        )

    def cargo(slab):
        span = slab_rows(slab)
        return remote(
            own.at[span], far_own.at[span],
            cargo_send.at[slab], cargo_recv.at[slab], (far, me),
        )

    def side(step):
        if step:
            span, target = pl.ds(0, ready * SLAB), far_second
        else:
            span, target = pl.ds(middle * SLAB, early * SLAB), far_first
        return remote(
            hidden_ref.at[0, step, :, span], target,
            side_send.at[step], side_recv.at[step], (far, me),
        )

    for slab in range(middle, ready):
        early_cargo(slab).start()
    for step in range(2):
        side(step).start()

    @pl.when(me == 0)
    def _():
        for step in range(2):
            arriving[step, 0] = jnp.zeros(arriving.shape[2:], arriving.dtype)

    @pl.when(me == last)
    def _():
        for step in range(2):
            arriving[step, 1] = jnp.zeros(arriving.shape[2:], arriving.dtype)

    def place(chunk):
        return chunk % tiles, pl.ds(pl.multiple_of((chunk // tiles) * ROWS, ROWS), ROWS)

    def right_copy(step, chunk):
        tile, rows = place(chunk)
        return remote(
            out_right.at[tile, rows], arriving.at[step, 0, tile, rows],
            right_send.at[step, chunk], right_recv.at[step, chunk],
            (replica, lax.rem(me + 1, count)),
        )

    def left_copy(step, chunk):
        tile, rows = place(chunk)
        return remote(
            out_left.at[tile, rows], arriving.at[step, 1, tile, rows],
            left_send.at[step, chunk], left_recv.at[step, chunk],
            (replica, lax.rem(me + count - 1, count)),
        )

    block = ROWS // tiles
    lag = tiles - 1 + jnp.maximum(me, last - me)

    def chain(step):
        def turn(now, _):
            @pl.when(now < chunks)
            def _():
                if step == 0:

                    @pl.when(now < tiles)
                    def _():
                        tile_copy(now).wait()

                tile, rows = place(now)
                terms[tile, rows, :] = factor * jnp.dot(
                    rows_in[step, rows, :], own[:, columns_of(tile)],
                    preferred_element_type=jnp.float32,
                )

            rightward = now - me

            @pl.when((rightward >= 0) & (rightward < chunks))
            def _():
                @pl.when(me > 0)
                def _():
                    right_copy(step, rightward).wait_recv()

                @pl.when(me < last)
                def _():
                    tile, rows = place(rightward)
                    total = terms[tile, rows, :] + arriving[step, 0, tile, rows, :].astype(jnp.float32)
                    out_right[tile, rows, :] = total.astype(jnp.bfloat16)
                    right_copy(step, rightward).start()

            leftward = now - (last - me)

            @pl.when((leftward >= 0) & (leftward < chunks))
            def _():
                @pl.when(me < last)
                def _():
                    left_copy(step, leftward).wait_recv()

                @pl.when(me > 0)
                def _():
                    tile, rows = place(leftward)
                    total = terms[tile, rows, :] + arriving[step, 1, tile, rows, :].astype(jnp.float32)
                    out_left[tile, rows, :] = total.astype(jnp.bfloat16)
                    left_copy(step, leftward).start()

            index = now - lag

            @pl.when((index >= 0) & (index < chunks))
            def _():
                @pl.when(index == 0)
                def _():
                    target_copy(step).wait()

                rows = pl.ds(pl.multiple_of(index * block, block), block)
                outputs = jnp.concatenate(
                    [
                        terms[tile, rows, :]
                        + arriving[step, 0, tile, rows, :].astype(jnp.float32)
                        + arriving[step, 1, tile, rows, :].astype(jnp.float32)
                        for tile in range(tiles)
                    ],
                    axis=1,
                )
                grads[step, rows, :] = norm_backward(outputs, goal[step, rows, :], gain_ref[...])

            return 0

        hidden_copy(step).wait()
        lax.fori_loop(0, chunks + tiles - 1 + last, turn, 0)

    def drain(step):
        def sent(chunk, _):
            @pl.when(me < last)
            def _():
                right_copy(step, chunk).wait_send()

            @pl.when(me > 0)
            def _():
                left_copy(step, chunk).wait_send()

            return 0

        lax.fori_loop(0, chunks, sent, 0)

    part = tokens // count

    def part_rows(index):
        return pl.ds(pl.multiple_of(index * part, part), part)

    def across(step):
        return remote(
            grads.at[step, part_rows(me)], far_grads.at[step, part_rows(me)],
            across_send.at[step], across_recv.at[step], (far, me),
        )

    def pass_right(step, index):
        piece = far_grads.at[step, part_rows(index)]
        return remote(
            piece, piece, share_right.at[step, index], share_recv.at[step, index],
            (replica, lax.rem(me + 1, count)),
        )

    def pass_left(step, index):
        piece = far_grads.at[step, part_rows(index)]
        return remote(
            piece, piece, share_left.at[step, index], share_recv.at[step, index],
            (replica, lax.rem(me + count - 1, count)),
        )

    def gather_first(step):
        across(step).wait_recv()

        @pl.when(me < last)
        def _():
            pass_right(step, me).start()

        @pl.when(me > 0)
        def _():
            pass_left(step, me).start()

    def gather_rest(step):
        def hop(distance, _):
            lower, upper = me - distance, me + distance

            @pl.when(lower >= 0)
            def _():
                pass_right(step, lower).wait_recv()

                @pl.when(me < last)
                def _():
                    pass_right(step, lower).start()

            @pl.when(upper <= last)
            def _():
                pass_left(step, upper).wait_recv()

                @pl.when(me > 0)
                def _():
                    pass_left(step, upper).start()

            return 0

        lax.fori_loop(1, count, hop, 0)

    def gather_sent(step):
        def hop(index, _):
            @pl.when((me < last) & (index <= me))
            def _():
                pass_right(step, index).wait_send()

            @pl.when((me > 0) & (index >= me))
            def _():
                pass_left(step, index).wait_send()

            return 0

        lax.fori_loop(0, count, hop, 0)

    def descended(block_rows, hidden_columns, gradient):
        grad_weight = (factor * contract_rows(hidden_columns, gradient)).astype(jnp.bfloat16)
        return (
            block_rows.astype(jnp.float32) - learn_rate * grad_weight.astype(jnp.float32)
        ).astype(jnp.bfloat16)

    def descend_own(step, slab):
        span = slab_rows(slab)
        own[span, :] = descended(own[span, :], rows_in[step, :, span], grads[step])

    def near_copy(slab):
        span = slab_rows(slab)
        return remote(
            own.at[span], theirs.at[span], near_send.at[slab], near_recv.at[slab], (near, me)
        )

    def swap(slab):
        index = slab - middle
        return remote(
            far_own.at[slab_rows(slab)], crossed.at[slab_rows(index)],
            swap_send.at[index], swap_recv.at[index], (near, me),
        )

    def store(slab):
        span = slab_rows(slab)
        return pltpu.make_async_copy(own.at[span], new_ref.at[span], store_sem.at[slab])

    def loop(low, high, body):
        def run(index, _):
            body(index)
            return 0

        lax.fori_loop(low, high, run, 0)

    chain(0)
    across(0).start()

    def offer(slab):
        descend_own(0, slab)
        near_copy(slab).start()

    def settle(slab):
        span = slab_rows(slab)
        near_copy(slab).wait()
        own[span, :] = mix(own_mix, own[span, :], theirs[span, :])

        @pl.when(slab < middle)
        def _():
            cargo(slab).start()

    loop(0, slabs, offer)
    loop(0, slabs, settle)
    drain(0)

    chain(1)
    across(1).start()
    gather_first(0)

    def give(slab):
        descend_own(1, slab)
        cargo(slab).start()

    loop(ready, slabs, give)
    gather_rest(0)

    def keep(slab):
        @pl.when(slab < middle)
        def _():
            cargo(slab).wait_send()

        descend_own(1, slab)

    loop(0, ready, keep)

    side(0).wait_recv()

    def replay(slab):
        span = slab_rows(slab)
        early_cargo(slab).wait_recv()
        far_own[span, :] = descended(
            far_own[span, :], far_first[:, slab_rows(slab - middle)], far_grads[0]
        )
        swap(slab).start()

    def level(slab):
        span = slab_rows(slab)
        swap(slab).wait()
        far_own[span, :] = mix(far_mix, far_own[span, :], crossed[slab_rows(slab - middle), :])

    loop(middle, ready, replay)
    loop(middle, ready, level)

    gather_first(1)
    gather_rest(1)
    side(1).wait_recv()

    def join(slab):
        span = slab_rows(slab)

        @pl.when(slab < middle)
        def _():
            cargo(slab).wait_recv()

        other = descended(far_own[span, :], far_second[:, span], far_grads[1])
        own[span, :] = mix(end_mix, own[span, :], other)
        store(slab).start()

    loop(0, ready, join)

    def finish(slab):
        span = slab_rows(slab)
        cargo(slab).wait()
        own[span, :] = mix(end_mix, own[span, :], far_own[span, :])
        store(slab).start()

    loop(ready, slabs, finish)

    drain(1)
    for step in range(2):
        gather_sent(step)
        across(step).wait_send()
        side(step).wait_send()
    for slab in range(middle, ready):
        early_cargo(slab).wait_send()
    loop(0, slabs, lambda slab: store(slab).wait())


def on_device(weights, hidden, targets, norm_gain, stragglers):
    _, depth, features = weights.shape
    tokens = hidden.shape[2]
    count = lax.axis_size("tensor")
    tiles = features // TILE
    chunks = tiles * (tokens // ROWS)
    slabs = depth // SLAB
    middle, early = round(slabs * MIDDLE), round(slabs * EARLY)
    anywhere = pl.BlockSpec(memory_space=pl.ANY)

    def buffer(*shape, dtype=jnp.bfloat16):
        return pltpu.VMEM(shape, dtype)

    def sems(*shape):
        return pltpu.SemaphoreType.DMA(shape)

    return pl.pallas_call(
        functools.partial(steps_kernel, middle, early),
        out_shape=jax.ShapeDtypeStruct((depth, features), weights.dtype),
        in_specs=[anywhere] * 3
        + [pl.BlockSpec(memory_space=pltpu.VMEM), pl.BlockSpec(memory_space=pltpu.SMEM)],
        out_specs=anywhere,
        scratch_shapes=[
            buffer(depth, features),
            buffer(depth, features),
            buffer(depth, features),
            buffer(early * SLAB, features),
            buffer(2, tokens, depth),
            buffer(tokens, early * SLAB),
            buffer(tokens, (middle + early) * SLAB),
            buffer(2, tokens, features),
            buffer(tiles, tokens, TILE, dtype=jnp.float32),
            buffer(2, 2, tiles, tokens, TILE),
            buffer(tiles, tokens, TILE),
            buffer(tiles, tokens, TILE),
            buffer(2, tokens, features),
            buffer(2, tokens, features),
            sems(tiles),
            sems(2, 2),
            *[sems(2, chunks)] * 4,
            *[sems(slabs)] * 4,
            *[sems(early)] * 2,
            *[sems(2)] * 4,
            *[sems(2, count)] * 3,
            sems(slabs),
        ],
        compiler_params=pltpu.CompilerParams(
            collective_id=0, has_side_effects=True, vmem_limit_bytes=63 << 20
        ),
    )(weights, hidden, targets, norm_gain[None], stragglers)[None]


def solution(mesh):
    placed = (
        P("replica", "tensor", None),
        P("replica", None, None, "tensor"),
        P("replica", None, None, None),
        P(),
        P(),
    )
    return jax.shard_map(
        on_device,
        mesh=mesh,
        in_specs=placed,
        out_specs=P("replica", "tensor", None),
        check_vma=False,
    )
```

time: 325 us -> 264 us (0.81)
  the two profiles are of different devices: /device:TPU:0 before, /device:TPU:1 now
where the time goes in v1:
time: 264 us; the launch traced here: 259 us
  Pallas kernels  252 us (95%)
  local copies, waits for them, and re-layouts  7.53 us (3%)
    pallas_call x1, Pallas kernels, on_device(): pl.pallas_call(functools.partial(steps_kernel, middle, early), out_shape=...  252 us
    unnamed x1, local copies, waits for them, and re-layouts  7.53 us

profile of v1, /device:TPU:1, one launch (start us, length us, event | category | flops | bytes accessed | tf_op | source)
XLA Modules:
  0.0 259.5 jit_solution(2107155815566205624)
XLA Ops:
  0.0 251.9 %shard_map.55 = bf16[1792,2048]{1,0:T(8,128)(2,1)} custom-call(bf16[1,1792,2048]{2,1,0:T(8,128)(2,1)} %refs_0_.1, bf16[1,2,512,1792]{3,2,1,0:T(8,128)(2,1)} %refs_1_.1, bf16[1,2,512,2048]{3,2,1,0:T(8,128)(2,1)} %refs_2_.1, f32[1,2048]{1,0:T(1,128)} %bitcast.3, s32[2,8]{1,0:T(2,128)} %refs_4_.1), custom_call_target="tpu_custom_call" | custom-call | tf_op jit(solution)/shard_map/pallas_call | solution.py:479
  251.9 7.5 %copy.7 = bf16[1,1792,2048]{2,1,0:T(8,128)(2,1)} copy(bf16[1,1792,2048]{2,1,0:T(8,128)(2,1)} %bitcast.2) | data formatting | bytes 14680064

commit v2 on v1

--- a/solution.py
+++ b/solution.py
@@ -12,9 +12,10 @@
 
 MESH = pl.DeviceIdType.MESH
 TILE = 512
-ROWS = 128
+ROWS = 64
+LAG = 3
 SLAB = 128
-MIDDLE = 4 / 14
+MIDDLE = 5 / 14
 EARLY = 3 / 14
 
 
@@ -172,7 +173,7 @@
         )
 
     block = ROWS // tiles
-    lag = tiles - 1 + jnp.maximum(me, last - me)
+    lag = tiles - 1 + LAG * jnp.maximum(me, last - me)
 
     def chain(step):
         def turn(now, _):
@@ -190,7 +191,7 @@
                     preferred_element_type=jnp.float32,
                 )
 
-            rightward = now - me
+            rightward = now - LAG * me
 
             @pl.when((rightward >= 0) & (rightward < chunks))
             def _():
@@ -205,7 +206,7 @@
                     out_right[tile, rows, :] = total.astype(jnp.bfloat16)
                     right_copy(step, rightward).start()
 
-            leftward = now - (last - me)
+            leftward = now - LAG * (last - me)
 
             @pl.when((leftward >= 0) & (leftward < chunks))
             def _():
@@ -243,7 +244,7 @@
             return 0
 
         hidden_copy(step).wait()
-        lax.fori_loop(0, chunks + tiles - 1 + last, turn, 0)
+        lax.fori_loop(0, chunks + tiles - 1 + LAG * last, turn, 0)
 
     def drain(step):
         def sent(chunk, _):
@@ -396,6 +397,7 @@
         cargo(slab).start()
 
     loop(ready, slabs, give)
+    gather_first(1)
     gather_rest(0)
 
     def keep(slab):
@@ -424,8 +426,6 @@
 
     loop(middle, ready, replay)
     loop(middle, ready, level)
-
-    gather_first(1)
     gather_rest(1)
     side(1).wait_recv()
 

time: 264 us -> 231 us (0.88)
  Pallas kernels: 252 us -> 222 us
    pallas_call x1, Pallas kernels: 252 us -> 222 us  [on_device(): pl.pallas_call(functools.partial(steps_kernel, middle, early), out_shape=...]
where the time goes in v2:
time: 231 us; the launch traced here: 229 us
  Pallas kernels  222 us (96%)
  local copies, waits for them, and re-layouts  7.53 us (3%)
    pallas_call x1, Pallas kernels, on_device(): pl.pallas_call(functools.partial(steps_kernel, middle, early), out_shape=...  222 us
    unnamed x1, local copies, waits for them, and re-layouts  7.53 us

profile of v2, /device:TPU:1, one launch (start us, length us, event | category | flops | bytes accessed | tf_op | source)
XLA Modules:
  0.0 229.1 jit_solution(16371049489436428558)
XLA Ops:
  0.0 221.5 %shard_map.55 = bf16[1792,2048]{1,0:T(8,128)(2,1)} custom-call(bf16[1,1792,2048]{2,1,0:T(8,128)(2,1)} %refs_0_.1, bf16[1,2,512,1792]{3,2,1,0:T(8,128)(2,1)} %refs_1_.1, bf16[1,2,512,2048]{3,2,1,0:T(8,128)(2,1)} %refs_2_.1, f32[1,2048]{1,0:T(1,128)} %bitcast.3, s32[2,8]{1,0:T(2,128)} %refs_4_.1), custom_call_target="tpu_custom_call" | custom-call | tf_op jit(solution)/shard_map/pallas_call | solution.py:479
  221.6 7.5 %copy.7 = bf16[1,1792,2048]{2,1,0:T(8,128)(2,1)} copy(bf16[1,1792,2048]{2,1,0:T(8,128)(2,1)} %bitcast.2) | data formatting | bytes 14680064

commit v3 on v2

--- a/solution.py
+++ b/solution.py
@@ -15,6 +15,7 @@
 ROWS = 64
 LAG = 3
 SLAB = 128
+PAIR = 1
 MIDDLE = 5 / 14
 EARLY = 3 / 14
 
@@ -39,13 +40,13 @@
 
 
 def steps_kernel(middle, early, *refs):
-    weights_ref, hidden_ref, targets_ref, gain_ref, late_ref, new_ref = refs[:6]
-    own, theirs, far_own, crossed, rows_in, far_first, far_second = refs[6:13]
-    goal, terms, arriving, out_right, out_left, grads, far_grads = refs[13:20]
-    tile_load, load, right_send, right_recv, left_send, left_recv = refs[20:26]
-    near_send, near_recv, cargo_send, cargo_recv, swap_send, swap_recv = refs[26:32]
-    side_send, side_recv, across_send, across_recv = refs[32:36]
-    share_right, share_left, share_recv, store_sem = refs[36:]
+    weights_ref, hidden_ref, targets_ref, gain_ref, late_ref, own = refs[:6]
+    theirs, far_own, crossed, rows_in, far_first, far_second = refs[6:12]
+    goal, terms, arriving, out_right, out_left, grads, far_grads = refs[12:19]
+    tile_load, load, right_send, right_recv, left_send, left_recv = refs[19:25]
+    near_send, near_recv, cargo_send, cargo_recv, swap_send, swap_recv = refs[25:31]
+    side_send, side_recv, across_send, across_recv = refs[31:35]
+    share_right, share_left, share_recv = refs[35:]
 
     count = lax.axis_size("tensor")
     me = lax.axis_index("tensor")
@@ -100,10 +101,17 @@
     barrier = pltpu.get_barrier_semaphore()
     pl.semaphore_signal(barrier, inc=1, device_id=(far, me), device_id_type=MESH)
     pl.semaphore_signal(barrier, inc=1, device_id=(near, me), device_id_type=MESH)
-    for hop in range(1, count):
-        peer = lax.rem(me + hop, count)
-        pl.semaphore_signal(barrier, inc=1, device_id=(replica, peer), device_id_type=MESH)
-    pl.semaphore_wait(barrier, count + 1)
+
+    @pl.when(me > 0)
+    def _():
+        pl.semaphore_signal(barrier, inc=1, device_id=(replica, me - 1), device_id_type=MESH)
+
+    @pl.when(me < last)
+    def _():
+        pl.semaphore_signal(barrier, inc=1, device_id=(replica, me + 1), device_id_type=MESH)
+
+    ends = jnp.where((me == 0) | (me == last), 1, 2)
+    pl.semaphore_wait(barrier, 2 + ends)
 
     def slab_rows(slab):
         return pl.ds(pl.multiple_of(slab * SLAB, SLAB), SLAB)
@@ -160,7 +168,7 @@
         tile, rows = place(chunk)
         return remote(
             out_right.at[tile, rows], arriving.at[step, 0, tile, rows],
-            right_send.at[step, chunk], right_recv.at[step, chunk],
+            right_send.at[step], right_recv.at[chunk],
             (replica, lax.rem(me + 1, count)),
         )
 
@@ -168,7 +176,7 @@
         tile, rows = place(chunk)
         return remote(
             out_left.at[tile, rows], arriving.at[step, 1, tile, rows],
-            left_send.at[step, chunk], left_recv.at[step, chunk],
+            left_send.at[step], left_recv.at[chunk],
             (replica, lax.rem(me + count - 1, count)),
         )
 
@@ -247,18 +255,19 @@
         lax.fori_loop(0, chunks + tiles - 1 + LAG * last, turn, 0)
 
     def drain(step):
-        def sent(chunk, _):
-            @pl.when(me < last)
-            def _():
-                right_copy(step, chunk).wait_send()
-
-            @pl.when(me > 0)
-            def _():
-                left_copy(step, chunk).wait_send()
-
-            return 0
-
-        lax.fori_loop(0, chunks, sent, 0)
+        @pl.when(me < last)
+        def _():
+            remote(
+                out_right, arriving.at[step, 0], right_send.at[step], right_recv.at[0],
+                (replica, lax.rem(me + 1, count)),
+            ).wait_send()
+
+        @pl.when(me > 0)
+        def _():
+            remote(
+                out_left, arriving.at[step, 1], left_send.at[step], left_recv.at[0],
+                (replica, lax.rem(me + count - 1, count)),
+            ).wait_send()
 
     part = tokens // count
 
@@ -296,7 +305,7 @@
         def _():
             pass_left(step, me).start()
 
-    def gather_rest(step):
+    def gather_rest(step, low, high):
         def hop(distance, _):
             lower, upper = me - distance, me + distance
 
@@ -318,7 +327,7 @@
 
             return 0
 
-        lax.fori_loop(1, count, hop, 0)
+        lax.fori_loop(low, high, hop, 0)
 
     def gather_sent(step):
         def hop(index, _):
@@ -340,14 +349,16 @@
             block_rows.astype(jnp.float32) - learn_rate * grad_weight.astype(jnp.float32)
         ).astype(jnp.bfloat16)
 
-    def descend_own(step, slab):
-        span = slab_rows(slab)
+    def descend_own(step, span):
         own[span, :] = descended(own[span, :], rows_in[step, :, span], grads[step])
 
-    def near_copy(slab):
-        span = slab_rows(slab)
-        return remote(
-            own.at[span], theirs.at[span], near_send.at[slab], near_recv.at[slab], (near, me)
+    def pair_rows(pair):
+        return pl.ds(pl.multiple_of(pair * PAIR * SLAB, PAIR * SLAB), PAIR * SLAB)
+
+    def near_copy(pair):
+        span = pair_rows(pair)
+        return remote(
+            own.at[span], theirs.at[span], near_send.at[pair], near_recv.at[pair], (near, me)
         )
 
     def swap(slab):
@@ -356,10 +367,6 @@
             far_own.at[slab_rows(slab)], crossed.at[slab_rows(index)],
             swap_send.at[index], swap_recv.at[index], (near, me),
         )
-
-    def store(slab):
-        span = slab_rows(slab)
-        return pltpu.make_async_copy(own.at[span], new_ref.at[span], store_sem.at[slab])
 
     def loop(low, high, body):
         def run(index, _):
@@ -371,21 +378,23 @@
     chain(0)
     across(0).start()
 
-    def offer(slab):
-        descend_own(0, slab)
-        near_copy(slab).start()
-
-    def settle(slab):
-        span = slab_rows(slab)
-        near_copy(slab).wait()
+    def offer(pair):
+        descend_own(0, pair_rows(pair))
+        near_copy(pair).start()
+
+    def settle(pair):
+        span = pair_rows(pair)
+        near_copy(pair).wait()
         own[span, :] = mix(own_mix, own[span, :], theirs[span, :])
-
-        @pl.when(slab < middle)
-        def _():
-            cargo(slab).start()
-
-    loop(0, slabs, offer)
-    loop(0, slabs, settle)
+        for index in range(PAIR):
+            slab = pair * PAIR + index
+
+            @pl.when(slab < middle)
+            def _():
+                cargo(slab).start()
+
+    loop(0, slabs // PAIR, offer)
+    loop(0, slabs // PAIR, settle)
     drain(0)
 
     chain(1)
@@ -393,19 +402,20 @@
     gather_first(0)
 
     def give(slab):
-        descend_own(1, slab)
+        descend_own(1, slab_rows(slab))
         cargo(slab).start()
 
     loop(ready, slabs, give)
+    gather_rest(0, 1, 2)
     gather_first(1)
-    gather_rest(0)
+    gather_rest(0, 2, count)
 
     def keep(slab):
         @pl.when(slab < middle)
         def _():
             cargo(slab).wait_send()
 
-        descend_own(1, slab)
+        descend_own(1, slab_rows(slab))
 
     loop(0, ready, keep)
 
@@ -426,7 +436,7 @@
 
     loop(middle, ready, replay)
     loop(middle, ready, level)
-    gather_rest(1)
+    gather_rest(1, 1, count)
     side(1).wait_recv()
 
     def join(slab):
@@ -438,7 +448,6 @@
 
         other = descended(far_own[span, :], far_second[:, span], far_grads[1])
         own[span, :] = mix(end_mix, own[span, :], other)
-        store(slab).start()
 
     loop(0, ready, join)
 
@@ -446,7 +455,6 @@
         span = slab_rows(slab)
         cargo(slab).wait()
         own[span, :] = mix(end_mix, own[span, :], far_own[span, :])
-        store(slab).start()
 
     loop(ready, slabs, finish)
 
@@ -457,7 +465,6 @@
         side(step).wait_send()
     for slab in range(middle, ready):
         early_cargo(slab).wait_send()
-    loop(0, slabs, lambda slab: store(slab).wait())
 
 
 def on_device(weights, hidden, targets, norm_gain, stragglers):
@@ -478,12 +485,11 @@
 
     return pl.pallas_call(
         functools.partial(steps_kernel, middle, early),
-        out_shape=jax.ShapeDtypeStruct((depth, features), weights.dtype),
+        out_shape=pltpu.VMEM((depth, features), weights.dtype),
         in_specs=[anywhere] * 3
         + [pl.BlockSpec(memory_space=pltpu.VMEM), pl.BlockSpec(memory_space=pltpu.SMEM)],
-        out_specs=anywhere,
+        out_specs=pl.BlockSpec(memory_space=pltpu.VMEM),
         scratch_shapes=[
-            buffer(depth, features),
             buffer(depth, features),
             buffer(depth, features),
             buffer(early * SLAB, features),
@@ -499,15 +505,18 @@
             buffer(2, tokens, features),
             sems(tiles),
             sems(2, 2),
-            *[sems(2, chunks)] * 4,
-            *[sems(slabs)] * 4,
+            sems(2),
+            sems(chunks),
+            sems(2),
+            sems(chunks),
+            *[sems(slabs // PAIR)] * 2,
+            *[sems(slabs)] * 2,
             *[sems(early)] * 2,
             *[sems(2)] * 4,
             *[sems(2, count)] * 3,
-            sems(slabs),
         ],
         compiler_params=pltpu.CompilerParams(
-            collective_id=0, has_side_effects=True, vmem_limit_bytes=63 << 20
+            collective_id=0, has_side_effects=True, vmem_limit_bytes=56 << 20
         ),
     )(weights, hidden, targets, norm_gain[None], stragglers)[None]
 

time: 231 us -> 222 us (0.961)
  Pallas kernels: 222 us -> 217 us
  local copies, waits for them, and re-layouts: 7.53 us -> 3.05 us
    pallas_call x1, Pallas kernels: 222 us -> 217 us  [on_device(): pl.pallas_call(functools.partial(steps_kernel, middle, early), out_shape=...]
    unnamed x1, local copies, waits for them, and re-layouts: 7.53 us -> 3.05 us
where the time goes in v3:
time: 222 us; the launch traced here: 220 us
  Pallas kernels  217 us (98%)
  local copies, waits for them, and re-layouts  3.05 us (1%)
    pallas_call x1, Pallas kernels, on_device(): pl.pallas_call(functools.partial(steps_kernel, middle, early), out_shape=...  217 us

profile of v3, /device:TPU:1, one launch (start us, length us, event | category | flops | bytes accessed | tf_op | source)
XLA Modules:
  0.0 220.0 jit_solution(2781276041732771806)
XLA Ops:
  0.0 217.0 %shard_map.55 = bf16[1792,2048]{1,0:T(8,128)(2,1)S(1)} custom-call(bf16[1,1792,2048]{2,1,0:T(8,128)(2,1)} %refs_0_.1, bf16[1,2,512,1792]{3,2,1,0:T(8,128)(2,1)} %refs_1_.1, bf16[1,2,512,2048]{3,2,1,0:T(8,128)(2,1)} %refs_2_.1, f32[1,2048]{1,0:T(1,128)} %bitcast.3, s32[2,8]{1,0:T(2,128)} %refs_4_.1), custom_call_target="tpu_custom_call" | custom-call | tf_op jit(solution)/shard_map/pallas_call | solution.py:486
  217.0 3.1 %copy.7 = bf16[1,1792,2048]{2,1,0:T(8,128)(2,1)} copy(bf16[1,1792,2048]{2,1,0:T(8,128)(2,1)S(1)} %bitcast.2) | data formatting | bytes 14680064

commit v4 on v3

--- a/solution.py
+++ b/solution.py
@@ -13,11 +13,12 @@
 MESH = pl.DeviceIdType.MESH
 TILE = 512
 ROWS = 64
-LAG = 3
+LAG = (3, 5)
 SLAB = 128
 PAIR = 1
-MIDDLE = 5 / 14
 EARLY = 3 / 14
+MIDDLE = (0 / 14, 6 / 14)
+YIELD = 36
 
 
 def contract_rows(left, right):
@@ -39,14 +40,14 @@
     return index + bit - 2 * bit * ((index // bit) % 2)
 
 
-def steps_kernel(middle, early, *refs):
+def steps_kernel(early, middles, *refs):
     weights_ref, hidden_ref, targets_ref, gain_ref, late_ref, own = refs[:6]
     theirs, far_own, crossed, rows_in, far_first, far_second = refs[6:12]
     goal, terms, arriving, out_right, out_left, grads, far_grads = refs[12:19]
     tile_load, load, right_send, right_recv, left_send, left_recv = refs[19:25]
     near_send, near_recv, cargo_send, cargo_recv, swap_send, swap_recv = refs[25:31]
     side_send, side_recv, across_send, across_recv = refs[31:35]
-    share_right, share_left, share_recv = refs[35:]
+    share_right, share_left, share_recv, turn_sem = refs[35:]
 
     count = lax.axis_size("tensor")
     me = lax.axis_index("tensor")
@@ -60,7 +61,9 @@
     blocks = tokens // ROWS
     chunks = tiles * blocks
     slabs = depth // SLAB
-    ready = middle + early
+    parity = replica % 2
+    least, most = early + middles[0], early + middles[1]
+    ready = least + (most - least) * parity
     factor = (depth * count) ** (-0.5)
 
     def share_of(step, one, other):
@@ -136,20 +139,23 @@
             cargo_send.at[slab], cargo_recv.at[slab], (far, me),
         )
 
-    def side(step):
-        if step:
-            span, target = pl.ds(0, ready * SLAB), far_second
-        else:
-            span, target = pl.ds(middle * SLAB, early * SLAB), far_first
-        return remote(
-            hidden_ref.at[0, step, :, span], target,
-            side_send.at[step], side_recv.at[step], (far, me),
-        )
-
-    for slab in range(middle, ready):
+    def side(index):
+        step, low, high = ((0, 0, early), (1, 0, least), (1, least, most))[index]
+        target = far_second if step else far_first
+        span = pl.ds(low * SLAB, (high - low) * SLAB)
+        return remote(
+            hidden_ref.at[0, step, :, span], target.at[:, span],
+            side_send.at[index], side_recv.at[index], (far, me),
+        )
+
+    for slab in range(early):
         early_cargo(slab).start()
-    for step in range(2):
-        side(step).start()
+    for index in range(2):
+        side(index).start()
+
+    @pl.when(parity == 1)
+    def _():
+        side(2).start()
 
     @pl.when(me == 0)
     def _():
@@ -181,10 +187,17 @@
         )
 
     block = ROWS // tiles
-    lag = tiles - 1 + LAG * jnp.maximum(me, last - me)
 
     def chain(step):
+        lag = tiles - 1 + LAG[step] * jnp.maximum(me, last - me)
+
         def turn(now, _):
+            if step:
+
+                @pl.when((now == YIELD) & (parity == 0))
+                def _():
+                    pl.semaphore_signal(turn_sem, inc=1, device_id=(near, me), device_id_type=MESH)
+
             @pl.when(now < chunks)
             def _():
                 if step == 0:
@@ -199,7 +212,7 @@
                     preferred_element_type=jnp.float32,
                 )
 
-            rightward = now - LAG * me
+            rightward = now - LAG[step] * me
 
             @pl.when((rightward >= 0) & (rightward < chunks))
             def _():
@@ -214,7 +227,7 @@
                     out_right[tile, rows, :] = total.astype(jnp.bfloat16)
                     right_copy(step, rightward).start()
 
-            leftward = now - LAG * (last - me)
+            leftward = now - LAG[step] * (last - me)
 
             @pl.when((leftward >= 0) & (leftward < chunks))
             def _():
@@ -252,7 +265,13 @@
             return 0
 
         hidden_copy(step).wait()
-        lax.fori_loop(0, chunks + tiles - 1 + LAG * last, turn, 0)
+        if step:
+
+            @pl.when(parity == 1)
+            def _():
+                pl.semaphore_wait(turn_sem, 1)
+
+        lax.fori_loop(0, chunks + tiles - 1 + LAG[step] * last, turn, 0)
 
     def drain(step):
         @pl.when(me < last)
@@ -362,10 +381,9 @@
         )
 
     def swap(slab):
-        index = slab - middle
-        return remote(
-            far_own.at[slab_rows(slab)], crossed.at[slab_rows(index)],
-            swap_send.at[index], swap_recv.at[index], (near, me),
+        span = slab_rows(slab)
+        return remote(
+            far_own.at[span], crossed.at[span], swap_send.at[slab], swap_recv.at[slab], (near, me)
         )
 
     def loop(low, high, body):
@@ -389,7 +407,7 @@
         for index in range(PAIR):
             slab = pair * PAIR + index
 
-            @pl.when(slab < middle)
+            @pl.when((slab >= early) & (slab < ready))
             def _():
                 cargo(slab).start()
 
@@ -411,7 +429,7 @@
     gather_rest(0, 2, count)
 
     def keep(slab):
-        @pl.when(slab < middle)
+        @pl.when(slab >= early)
         def _():
             cargo(slab).wait_send()
 
@@ -425,24 +443,28 @@
         span = slab_rows(slab)
         early_cargo(slab).wait_recv()
         far_own[span, :] = descended(
-            far_own[span, :], far_first[:, slab_rows(slab - middle)], far_grads[0]
+            far_own[span, :], far_first[:, span], far_grads[0]
         )
         swap(slab).start()
 
     def level(slab):
         span = slab_rows(slab)
         swap(slab).wait()
-        far_own[span, :] = mix(far_mix, far_own[span, :], crossed[slab_rows(slab - middle), :])
-
-    loop(middle, ready, replay)
-    loop(middle, ready, level)
+        far_own[span, :] = mix(far_mix, far_own[span, :], crossed[span, :])
+
+    loop(0, early, replay)
+    loop(0, early, level)
     gather_rest(1, 1, count)
     side(1).wait_recv()
 
+    @pl.when(parity == 1)
+    def _():
+        side(2).wait_recv()
+
     def join(slab):
         span = slab_rows(slab)
 
-        @pl.when(slab < middle)
+        @pl.when(slab >= early)
         def _():
             cargo(slab).wait_recv()
 
@@ -463,7 +485,12 @@
         gather_sent(step)
         across(step).wait_send()
         side(step).wait_send()
-    for slab in range(middle, ready):
+
+    @pl.when(parity == 1)
+    def _():
+        side(2).wait_send()
+
+    for slab in range(early):
         early_cargo(slab).wait_send()
 
 
@@ -474,7 +501,8 @@
     tiles = features // TILE
     chunks = tiles * (tokens // ROWS)
     slabs = depth // SLAB
-    middle, early = round(slabs * MIDDLE), round(slabs * EARLY)
+    early = round(slabs * EARLY)
+    middles = [round(slabs * part) for part in MIDDLE]
     anywhere = pl.BlockSpec(memory_space=pl.ANY)
 
     def buffer(*shape, dtype=jnp.bfloat16):
@@ -484,7 +512,7 @@
         return pltpu.SemaphoreType.DMA(shape)
 
     return pl.pallas_call(
-        functools.partial(steps_kernel, middle, early),
+        functools.partial(steps_kernel, early, middles),
         out_shape=pltpu.VMEM((depth, features), weights.dtype),
         in_specs=[anywhere] * 3
         + [pl.BlockSpec(memory_space=pltpu.VMEM), pl.BlockSpec(memory_space=pltpu.SMEM)],
@@ -495,7 +523,7 @@
             buffer(early * SLAB, features),
             buffer(2, tokens, depth),
             buffer(tokens, early * SLAB),
-            buffer(tokens, (middle + early) * SLAB),
+            buffer(tokens, (early + middles[1]) * SLAB),
             buffer(2, tokens, features),
             buffer(tiles, tokens, TILE, dtype=jnp.float32),
             buffer(2, 2, tiles, tokens, TILE),
@@ -512,8 +540,10 @@
             *[sems(slabs // PAIR)] * 2,
             *[sems(slabs)] * 2,
             *[sems(early)] * 2,
-            *[sems(2)] * 4,
+            *[sems(3)] * 2,
+            *[sems(2)] * 2,
             *[sems(2, count)] * 3,
+            pltpu.SemaphoreType.REGULAR,
         ],
         compiler_params=pltpu.CompilerParams(
             collective_id=0, has_side_effects=True, vmem_limit_bytes=56 << 20

time: 222 us -> 216 us (0.973)
  Pallas kernels: 217 us -> 212 us
    pallas_call x1, Pallas kernels: 217 us -> 212 us  [on_device(): pl.pallas_call(functools.partial(steps_kernel, early, middles), out_shape...]
where the time goes in v4:
time: 216 us; the launch traced here: 215 us
  Pallas kernels  212 us (98%)
  local copies, waits for them, and re-layouts  3.05 us (1%)
    pallas_call x1, Pallas kernels, on_device(): pl.pallas_call(functools.partial(steps_kernel, early, middles), out_shape...  212 us

profile of v4, /device:TPU:1, one launch (start us, length us, event | category | flops | bytes accessed | tf_op | source)
XLA Modules:
  0.0 215.4 jit_solution(10641786756576081765)
XLA Ops:
  0.0 212.4 %shard_map.55 = bf16[1792,2048]{1,0:T(8,128)(2,1)S(1)} custom-call(bf16[1,1792,2048]{2,1,0:T(8,128)(2,1)} %refs_0_.1, bf16[1,2,512,1792]{3,2,1,0:T(8,128)(2,1)} %refs_1_.1, bf16[1,2,512,2048]{3,2,1,0:T(8,128)(2,1)} %refs_2_.1, f32[1,2048]{1,0:T(1,128)} %bitcast.3, s32[2,8]{1,0:T(2,128)} %refs_4_.1), custom_call_target="tpu_custom_call" | custom-call | tf_op jit(solution)/shard_map/pallas_call | solution.py:514
  212.4 3.1 %copy.7 = bf16[1,1792,2048]{2,1,0:T(8,128)(2,1)} copy(bf16[1,1792,2048]{2,1,0:T(8,128)(2,1)S(1)} %bitcast.2) | data formatting | bytes 14680064

commit v5 on v4

--- a/solution.py
+++ b/solution.py
@@ -15,10 +15,13 @@
 ROWS = 64
 LAG = (3, 5)
 SLAB = 128
-PAIR = 1
+PAIR = 2
 EARLY = 3 / 14
 MIDDLE = (0 / 14, 6 / 14)
 YIELD = 36
+GROUP = 2
+RING = 16
+DELAY = 2
 
 
 def contract_rows(left, right):
@@ -41,13 +44,13 @@
 
 
 def steps_kernel(early, middles, *refs):
-    weights_ref, hidden_ref, targets_ref, gain_ref, late_ref, own = refs[:6]
+    weights_ref, hidden_ref, targets_ref, gain_any, late_any, own = refs[:6]
     theirs, far_own, crossed, rows_in, far_first, far_second = refs[6:12]
     goal, terms, arriving, out_right, out_left, grads, far_grads = refs[12:19]
     tile_load, load, right_send, right_recv, left_send, left_recv = refs[19:25]
     near_send, near_recv, cargo_send, cargo_recv, swap_send, swap_recv = refs[25:31]
     side_send, side_recv, across_send, across_recv = refs[31:35]
-    share_right, share_left, share_recv, turn_sem = refs[35:]
+    share_right, share_left, share_recv, turn_sem, gain_ref, late_ref, small = refs[35:]
 
     count = lax.axis_size("tensor")
     me = lax.axis_index("tensor")
@@ -70,10 +73,6 @@
         late = (late_ref[step, one] != 0) | (late_ref[step, other] != 0)
         return jnp.where(late, 1.0, 0.5), jnp.where(late, 0.0, 0.5)
 
-    own_mix = share_of(0, replica, near)
-    far_mix = share_of(0, far, cross)
-    end_mix = share_of(1, replica, far)
-
     def mix(shares, one, other):
         return (
             one.astype(jnp.float32) * shares[0] + other.astype(jnp.float32) * shares[1]
@@ -94,24 +93,38 @@
     def target_copy(step):
         return pltpu.make_async_copy(targets_ref.at[0, step], goal.at[step], load.at[step, 1])
 
+    barrier = pltpu.get_barrier_semaphore()
+    pl.semaphore_signal(barrier, inc=1, device_id=(far, me), device_id_type=MESH)
+    pl.semaphore_signal(barrier, inc=1, device_id=(near, me), device_id_type=MESH)
+
+    @pl.when(me > 0)
+    def _():
+        pl.semaphore_signal(barrier, inc=1, device_id=(replica, me - 1), device_id_type=MESH)
+
+    @pl.when(me < last)
+    def _():
+        pl.semaphore_signal(barrier, inc=1, device_id=(replica, me + 1), device_id_type=MESH)
+
+    gain_copy = pltpu.make_async_copy(gain_any, gain_ref, small.at[0])
+    late_copy = pltpu.make_async_copy(late_any, late_ref, small.at[1])
     hidden_copy(0).start()
     for tile in range(tiles):
         tile_copy(tile).start()
     target_copy(0).start()
+    gain_copy.start()
+    late_copy.start()
     hidden_copy(1).start()
     target_copy(1).start()
 
-    barrier = pltpu.get_barrier_semaphore()
-    pl.semaphore_signal(barrier, inc=1, device_id=(far, me), device_id_type=MESH)
-    pl.semaphore_signal(barrier, inc=1, device_id=(near, me), device_id_type=MESH)
-
-    @pl.when(me > 0)
-    def _():
-        pl.semaphore_signal(barrier, inc=1, device_id=(replica, me - 1), device_id_type=MESH)
-
-    @pl.when(me < last)
-    def _():
-        pl.semaphore_signal(barrier, inc=1, device_id=(replica, me + 1), device_id_type=MESH)
+    @pl.when(me == 0)
+    def _():
+        for step in range(2):
+            arriving[step, 0] = jnp.zeros(arriving.shape[2:], arriving.dtype)
+
+    @pl.when(me == last)
+    def _():
+        for step in range(2):
+            arriving[step, 1] = jnp.zeros(arriving.shape[2:], arriving.dtype)
 
     ends = jnp.where((me == 0) | (me == last), 1, 2)
     pl.semaphore_wait(barrier, 2 + ends)
@@ -157,16 +170,6 @@
     def _():
         side(2).start()
 
-    @pl.when(me == 0)
-    def _():
-        for step in range(2):
-            arriving[step, 0] = jnp.zeros(arriving.shape[2:], arriving.dtype)
-
-    @pl.when(me == last)
-    def _():
-        for step in range(2):
-            arriving[step, 1] = jnp.zeros(arriving.shape[2:], arriving.dtype)
-
     def place(chunk):
         return chunk % tiles, pl.ds(pl.multiple_of((chunk // tiles) * ROWS, ROWS), ROWS)
 
@@ -174,7 +177,7 @@
         tile, rows = place(chunk)
         return remote(
             out_right.at[tile, rows], arriving.at[step, 0, tile, rows],
-            right_send.at[step], right_recv.at[chunk],
+            right_send.at[step], right_recv.at[chunk % RING],
             (replica, lax.rem(me + 1, count)),
         )
 
@@ -182,7 +185,7 @@
         tile, rows = place(chunk)
         return remote(
             out_left.at[tile, rows], arriving.at[step, 1, tile, rows],
-            left_send.at[step], left_recv.at[chunk],
+            left_send.at[step], left_recv.at[chunk % RING],
             (replica, lax.rem(me + count - 1, count)),
         )
 
@@ -198,7 +201,7 @@
                 def _():
                     pl.semaphore_signal(turn_sem, inc=1, device_id=(near, me), device_id_type=MESH)
 
-            @pl.when(now < chunks)
+            @pl.when((now < chunks) & ((now // tiles) % GROUP == 0))
             def _():
                 if step == 0:
 
@@ -206,7 +209,8 @@
                     def _():
                         tile_copy(now).wait()
 
-                tile, rows = place(now)
+                tile = now % tiles
+                rows = pl.ds(pl.multiple_of((now // tiles) * ROWS, GROUP * ROWS), GROUP * ROWS)
                 terms[tile, rows, :] = factor * jnp.dot(
                     rows_in[step, rows, :], own[:, columns_of(tile)],
                     preferred_element_type=jnp.float32,
@@ -249,6 +253,8 @@
                 @pl.when(index == 0)
                 def _():
                     target_copy(step).wait()
+                    if step == 0:
+                        gain_copy.wait()
 
                 rows = pl.ds(pl.multiple_of(index * block, block), block)
                 outputs = jnp.concatenate(
@@ -395,6 +401,10 @@
 
     chain(0)
     across(0).start()
+    late_copy.wait()
+    own_mix = share_of(0, replica, near)
+    far_mix = share_of(0, far, cross)
+    end_mix = share_of(1, replica, far)
 
     def offer(pair):
         descend_own(0, pair_rows(pair))
@@ -411,8 +421,16 @@
             def _():
                 cargo(slab).start()
 
-    loop(0, slabs // PAIR, offer)
-    loop(0, slabs // PAIR, settle)
+    def trade(pair):
+        @pl.when(pair < slabs // PAIR)
+        def _():
+            offer(pair)
+
+        @pl.when(pair >= DELAY)
+        def _():
+            settle(pair - DELAY)
+
+    loop(0, slabs // PAIR + DELAY, trade)
     drain(0)
 
     chain(1)
@@ -514,8 +532,7 @@
     return pl.pallas_call(
         functools.partial(steps_kernel, early, middles),
         out_shape=pltpu.VMEM((depth, features), weights.dtype),
-        in_specs=[anywhere] * 3
-        + [pl.BlockSpec(memory_space=pltpu.VMEM), pl.BlockSpec(memory_space=pltpu.SMEM)],
+        in_specs=[anywhere] * 5,
         out_specs=pl.BlockSpec(memory_space=pltpu.VMEM),
         scratch_shapes=[
             buffer(depth, features),
@@ -534,9 +551,9 @@
             sems(tiles),
             sems(2, 2),
             sems(2),
-            sems(chunks),
+            sems(RING),
             sems(2),
-            sems(chunks),
+            sems(RING),
             *[sems(slabs // PAIR)] * 2,
             *[sems(slabs)] * 2,
             *[sems(early)] * 2,
@@ -544,6 +561,9 @@
             *[sems(2)] * 2,
             *[sems(2, count)] * 3,
             pltpu.SemaphoreType.REGULAR,
+            buffer(1, features, dtype=jnp.float32),
+            pltpu.SMEM(stragglers.shape, stragglers.dtype),
+            sems(2),
         ],
         compiler_params=pltpu.CompilerParams(
             collective_id=0, has_side_effects=True, vmem_limit_bytes=56 << 20

time: 216 us -> 214 us (level)
  no operation moved by 1% of the time
where the time goes in v5:
time: 214 us
  Pallas kernels  211 us (99%)
  local copies, waits for them, and re-layouts  3.05 us (1%)
    pallas_call x1, Pallas kernels, on_device(): pl.pallas_call(functools.partial(steps_kernel, early, middles), out_shape...  211 us

profile of v5, /device:TPU:1, one launch (start us, length us, event | category | flops | bytes accessed | tf_op | source)
XLA Modules:
  0.0 214.3 jit_solution(3676756439892959937)
XLA Ops:
  0.0 211.3 %shard_map.55 = bf16[1792,2048]{1,0:T(8,128)(2,1)S(1)} custom-call(bf16[1,1792,2048]{2,1,0:T(8,128)(2,1)} %refs_0_.1, bf16[1,2,512,1792]{3,2,1,0:T(8,128)(2,1)} %refs_1_.1, bf16[1,2,512,2048]{3,2,1,0:T(8,128)(2,1)} %refs_2_.1, f32[1,2048]{1,0:T(1,128)} %bitcast.3, s32[2,8]{1,0:T(2,128)} %refs_4_.1), custom_call_target="tpu_custom_call" | custom-call | tf_op jit(solution)/shard_map/pallas_call | solution.py:532
  211.3 3.1 %copy.7 = bf16[1,1792,2048]{2,1,0:T(8,128)(2,1)} copy(bf16[1,1792,2048]{2,1,0:T(8,128)(2,1)S(1)} %bitcast.2) | data formatting | bytes 14680064

commit v6 on v5

--- a/solution.py
+++ b/solution.py
@@ -17,7 +17,7 @@
 SLAB = 128
 PAIR = 2
 EARLY = 3 / 14
-MIDDLE = (0 / 14, 6 / 14)
+MIDDLE = (2 / 14, 4 / 14)
 YIELD = 36
 GROUP = 2
 RING = 16

time: 214 us -> 214 us (level)
  no operation moved by 1% of the time
where the time goes in v6:
time: 214 us
  Pallas kernels  211 us (99%)
  local copies, waits for them, and re-layouts  3.05 us (1%)
    pallas_call x1, Pallas kernels, on_device(): pl.pallas_call(functools.partial(steps_kernel, early, middles), out_shape...  211 us

profile of v6, /device:TPU:1, one launch (start us, length us, event | category | flops | bytes accessed | tf_op | source)
XLA Modules:
  0.0 214.3 jit_solution(16945110098906375994)
XLA Ops:
  0.0 211.2 %shard_map.55 = bf16[1792,2048]{1,0:T(8,128)(2,1)S(1)} custom-call(bf16[1,1792,2048]{2,1,0:T(8,128)(2,1)} %refs_0_.1, bf16[1,2,512,1792]{3,2,1,0:T(8,128)(2,1)} %refs_1_.1, bf16[1,2,512,2048]{3,2,1,0:T(8,128)(2,1)} %refs_2_.1, f32[1,2048]{1,0:T(1,128)} %bitcast.3, s32[2,8]{1,0:T(2,128)} %refs_4_.1), custom_call_target="tpu_custom_call" | custom-call | tf_op jit(solution)/shard_map/pallas_call | solution.py:532
  211.2 3.1 %copy.7 = bf16[1,1792,2048]{2,1,0:T(8,128)(2,1)} copy(bf16[1,1792,2048]{2,1,0:T(8,128)(2,1)S(1)} %bitcast.2) | data formatting | bytes 14680064
